TPU v7x, 32 devices: a whole 2x2x4 slice. The times are simulated.
32 devices in a mesh: row: 16 (over z, x, core), ch: 2 (over y).
Axes of the slice: x: 2, y: 2, z: 4, core: 2. Of those that a mesh axis runs over, the one named last changes fastest.
Arguments:
- pair_rep: float32 [256, 256, 128], P('row', 'ch'), may hold values from -6 to 6
- residue_mask: int32 [256], replicated, may hold values 0 or 1
- pair_gain: float32 [2, 128], replicated, may hold values from 0.5 to 1.5
- pair_shift: float32 [2, 128], replicated, may hold values from -3 to 3
- panel_weight: bfloat16 [2, 128, 512], replicated, may hold values from -0.5 to 0.5
- panel_bias: float32 [2, 512], replicated, may hold values from -3 to 3
- gate_weight: bfloat16 [2, 128, 128], replicated, may hold values from -0.5 to 0.5
- gate_bias: float32 [2, 128], replicated, may hold values from -3 to 3
- hidden_gain: float32 [2, 128], replicated, may hold values from 0.5 to 1.5
- hidden_shift: float32 [2, 128], replicated, may hold values from -3 to 3
- output_weight: bfloat16 [2, 128, 128], replicated, may hold values from -0.5 to 0.5
- output_bias: float32 [2, 128], replicated, may hold values from -3 to 3
Outputs:
- updated_pair: float32 [256, 256, 128], P('row', 'ch')
All inputs are finite; a program needn't handle non-finite values.
Results may differ from a plain program's by a relative error of at most 0.0039.
Values may be sent and summed in bfloat16 or wider, within the bound.
A program may use at most 64 MiB of HBM per device.

v0:
```python
import functools

import jax
import jax.numpy as jnp
from jax import lax
from jax.experimental import pallas as pl
from jax.experimental.pallas import tpu as pltpu
from jax.sharding import PartitionSpec as P

PAIR_EPSILON = 1e-05
HIDDEN_EPSILON = 1.0
MESH = pl.DeviceIdType.MESH
CHUNKS = 4
LEAD = 3
NAMES = (
    "pair",
    "mask",
    "pair_gain",
    "pair_shift",
    "panel_weight",
    "panel_bias",
    "gate_weight",
    "gate_bias",
    "hidden_gain",
    "hidden_shift",
    "output_weight",
    "output_bias",
)


def normalize(values, axis, epsilon, gain, shift):
    offset = values - jnp.mean(values, axis=axis, keepdims=True)
    spread = jnp.mean(offset * offset, axis=axis, keepdims=True)
    return (offset * lax.rsqrt(spread + epsilon) * gain + shift).astype(jnp.bfloat16)


def kernel(sizes, mask_smem, *refs):
    rows, cols, hidden, row_total, col_total, parts, chunks = sizes
    count = len(NAMES)
    sources = dict(zip(NAMES, refs[:count]))
    out_ref = refs[count]
    held = dict(zip(NAMES, refs[count + 1 : 2 * count + 1]))
    (
        weight_t,
        bias_t,
        affine_t,
        normed_ref,
        stage,
        stage_x,
        gate,
        send_ab,
        recv_a,
        recv_b,
        recv_ab,
        send_x0,
        send_x1,
        recv_x0,
        recv_x1,
        load_sem,
        a_send_sem,
        a_recv_sem,
        b_send_sem,
        b_recv_sem,
        ab_send_sem,
        ab_recv_sem,
        x_send_sem,
        x_recv_sem,
    ) = refs[2 * count + 1 :]
    devices = row_total * col_total
    row_part = row_total // parts
    members = row_part * col_total
    per_slot = hidden // members
    piece = per_slot // chunks
    wide = hidden // chunks
    total = row_total * rows
    part = total // parts
    my_row = lax.axis_index("row")
    my_col = lax.axis_index("ch")
    my_group = my_row // row_part
    my_place = lax.rem(my_row, row_part) * col_total + my_col

    loads = [
        pltpu.make_async_copy(sources[name], held[name], load_sem.at[at])
        for at, name in enumerate(NAMES)
    ]
    for load in loads:
        load.start()

    def partner(distance, step):
        group = lax.rem(my_group + distance, parts)
        place = lax.rem(my_place + step, members)
        return group * row_part + place // col_total, lax.rem(place, col_total), place

    def each(first, body):
        def step_body(step, carry):
            body(step)
            return carry

        steps = members - first
        unroll = max(d for d in (1, 4, 5) if steps % d == 0)
        lax.fori_loop(first, members, step_body, 0, unroll=unroll)

    barrier = pltpu.get_barrier_semaphore()
    for distance in range(parts):

        def greet(step):
            row, col, _ = partner(distance, step)
            pl.semaphore_signal(barrier, inc=1, device_id=(row, col), device_id_type=MESH)

        each(1 if distance == 0 else 0, greet)

    def wait_bytes(ref, sem):
        pltpu.make_async_copy(ref, ref, sem).wait()

    def remote(source, target, send_sem, recv_sem, row, col):
        pltpu.make_async_remote_copy(
            src_ref=source,
            dst_ref=target,
            send_sem=send_sem,
            recv_sem=recv_sem,
            device_id=(row, col),
            device_id_type=MESH,
        ).start()

    row_at = pl.multiple_of(my_row * rows, rows)
    near_at = pl.multiple_of(lax.rem(my_row, row_part) * rows, rows)
    col_at = pl.multiple_of(my_col * cols, cols)

    def panels(chunk, place):
        return pl.ds(chunk * wide + place * piece, piece)

    def send_panels(section, chunk):
        spot = pl.ds(chunk * piece, piece)
        if section == 0:
            a_to = recv_a.at[spot, pl.ds(near_at, rows), pl.ds(col_at, cols)]
            b_to = recv_b.at[spot, pl.ds(row_at, rows), pl.ds(col_at, cols)]

            def far(distance, step):
                row, col, place = partner(distance, step)
                source = send_ab.at[0, 1, panels(chunk, place)]
                remote(
                    source, b_to, b_send_sem.at[distance], b_recv_sem.at[chunk], row, col
                )

            def near(step):
                row, col, place = partner(0, step)
                source = send_ab.at[0, 0, panels(chunk, place)]
                remote(source, a_to, a_send_sem, a_recv_sem.at[chunk], row, col)

            for distance in range(parts - 1, -1, -1):
                each(1 if distance == 0 else 0, functools.partial(far, distance))
            each(1, near)
            own = panels(chunk, my_place)
            pltpu.make_async_copy(send_ab.at[0, 0, own], a_to, a_recv_sem.at[chunk]).start()
            pltpu.make_async_copy(send_ab.at[0, 1, own], b_to, b_recv_sem.at[chunk]).start()
        else:
            to = recv_ab.at[:, spot, pl.ds(near_at, rows), pl.ds(col_at, cols)]

            def both(step):
                row, col, place = partner(0, step)
                source = send_ab.at[1, :, panels(chunk, place)]
                remote(source, to, ab_send_sem, ab_recv_sem.at[chunk], row, col)

            each(1, both)
            own = send_ab.at[1, :, panels(chunk, my_place)]
            pltpu.make_async_copy(own, to, ab_recv_sem.at[chunk]).start()

    def wait_panels(section, chunk):
        spot = pl.ds(chunk * piece, piece)
        if section == 0:
            wait_bytes(recv_a.at[spot], a_recv_sem.at[chunk])
            wait_bytes(recv_b.at[spot], b_recv_sem.at[chunk])
        else:
            wait_bytes(recv_ab.at[:, spot], ab_recv_sem.at[chunk])

    def send_products(section, chunk):
        spot = pl.ds(chunk * piece, piece)
        lands = panels(chunk, my_place)

        def refs_of(row, col):
            to_row = row if section == 1 else lax.rem(row, row_part)
            at = pl.ds(pl.multiple_of(to_row * rows, rows), rows)
            along = pl.ds(pl.multiple_of(col * cols, cols), cols)
            if section == 0:
                return send_x0.at[spot, at, along], recv_x0.at[lands]
            return send_x1.at[spot, at, along], recv_x1.at[my_group, lands]

        def other(distance, step):
            row, col, _ = partner(distance, step)
            source, target = refs_of(row, col)
            remote(
                source,
                target,
                x_send_sem.at[section, distance],
                x_recv_sem.at[section, chunk],
                row,
                col,
            )

        for distance in range(parts - 1 if section == 1 else 0, -1, -1):
            each(1 if distance == 0 else 0, functools.partial(other, distance))
        source, target = refs_of(my_row, my_col)
        pltpu.make_async_copy(source, target, x_recv_sem.at[section, chunk]).start()

    def prepare(section):
        for block in range(4):
            span = slice(block * hidden, (block + 1) * hidden)
            turned = held["panel_weight"][section, :, span].astype(jnp.float32).T
            turned = turned.astype(jnp.bfloat16)
            biases = held["panel_bias"][pl.ds(section, 1), span]
            biases = jnp.broadcast_to(biases, (cols, hidden)).T
            for chunk in range(chunks):
                to = pl.ds((chunk * 4 + block) * wide, wide)
                weight_t[section, to, :] = turned[chunk * wide : (chunk + 1) * wide]
                bias_t[section, to, :] = biases[chunk * wide : (chunk + 1) * wide]

    def prepare_affine(section):
        for at, name in enumerate(("hidden_gain", "hidden_shift")):
            line = held[name][pl.ds(section, 1), :]
            affine_t[section, at] = jnp.broadcast_to(line, (cols, hidden)).T

    def norm_row(section, values):
        return normalize(
            values,
            1,
            PAIR_EPSILON,
            held["pair_gain"][pl.ds(section, 1), :],
            held["pair_shift"][pl.ds(section, 1), :],
        )

    early = [NAMES.index(name) for name in ("pair", "pair_gain", "pair_shift")]
    for at in early:
        loads[at].wait()

    def first_norm(r, carry):
        normed_ref[r] = norm_row(0, held["pair"][r])
        return carry

    lax.fori_loop(0, rows, first_norm, 0, unroll=min(rows, 16))
    for at in range(count):
        if at not in early:
            loads[at].wait()
    prepare(0)
    col_mask = held["mask"][pl.ds(my_col, 1), :].astype(jnp.float32)

    for section in range(2):
        current = held["pair"] if section == 0 else out_ref
        def make(chunk):

            def project(r, carry):
                span = pl.ds(chunk * 4 * wide, 4 * wide)
                features = lax.dot_general(
                    weight_t[section, span, :],
                    normed_ref[r],
                    (((1,), (1,)), ((), ())),
                    preferred_element_type=jnp.float32,
                )
                features = features + bias_t[section, span, :]
                mask = col_mask * mask_smem[my_row * rows + r].astype(jnp.float32)
                for which in range(2):
                    at = 2 * which * wide
                    panel = mask * jax.nn.sigmoid(features[at : at + wide])
                    panel = panel * features[at + wide : at + 2 * wide]
                    stage[which, pl.ds(r, wide, stride=rows), :] = panel
                return carry

            lax.fori_loop(0, rows, project, 0, unroll=min(rows, 16))
            for which in range(2):
                send_ab[section, which, pl.ds(chunk * wide, wide)] = (
                    stage[which].astype(jnp.bfloat16).reshape(wide, rows, cols)
                )
            if section == 0 and chunk == 0:
                pl.semaphore_wait(barrier, devices - 1)
            send_panels(section, chunk)

        def gates(r, carry):
            gate[r] = jax.nn.sigmoid(
                jnp.dot(
                    normed_ref[r],
                    held["gate_weight"][section],
                    preferred_element_type=jnp.float32,
                )
                + held["gate_bias"][pl.ds(section, 1), :]
            )
            return carry

        def multiply(chunk):
            wait_panels(section, chunk)
            for h in range(chunk * piece, (chunk + 1) * piece):
                if section == 0:
                    left, right, along, to = recv_a[h], recv_b[h], 1, send_x0
                else:
                    left, right, along, to = recv_ab[0, h], recv_ab[1, h], 0, send_x1
                to[h] = lax.dot_general(
                    left,
                    right,
                    (((along,), (along,)), ((), ())),
                    preferred_element_type=jnp.float32,
                ).astype(jnp.bfloat16)
            send_products(section, chunk)

        lead = chunks if section == 0 else min(LEAD, chunks)
        for chunk in range(lead):
            make(chunk)
        if section == 0:
            lax.fori_loop(0, rows, gates, 0, unroll=min(rows, 16))
            prepare(1)
            prepare_affine(0)
            prepare_affine(1)
        for chunk in range(chunks):
            multiply(chunk)
            if chunk + lead < chunks:
                make(chunk + lead)
        if section == 1:
            lax.fori_loop(0, rows, gates, 0, unroll=min(rows, 16))
        for chunk in range(chunks):
            spot = pl.ds(chunk * wide, wide)
            if section == 0:
                wait_bytes(recv_x0.at[spot], x_recv_sem.at[0, chunk])
                got = recv_x0[spot].astype(jnp.float32)
            else:
                wait_bytes(recv_x1.at[:, spot], x_recv_sem.at[1, chunk])
                got = recv_x1[0, spot].astype(jnp.float32)
                for other in range(1, parts):
                    got = got + recv_x1[other, spot].astype(jnp.float32)
            stage_x[pl.ds(chunk * wide * rows, wide * rows), :] = got.reshape(wide * rows, cols)

        def finish(r, carry):
            normed = normalize(
                stage_x[pl.ds(r, hidden, stride=rows), :],
                0,
                HIDDEN_EPSILON,
                affine_t[section, 0],
                affine_t[section, 1],
            )
            projected = lax.dot_general(
                normed,
                held["output_weight"][section],
                (((0,), (0,)), ((), ())),
                preferred_element_type=jnp.float32,
            )
            projected = projected + held["output_bias"][pl.ds(section, 1), :]
            updated = current[r] + gate[r] * projected
            out_ref[r] = updated
            if section == 0:
                normed_ref[r] = norm_row(1, updated)
            return carry

        lax.fori_loop(0, rows, finish, 0, unroll=min(rows, 16))

    one = hidden - per_slot
    wait_bytes(send_ab.at[0, 0, pl.ds(0, one)], a_send_sem)
    wait_bytes(send_ab.at[1, :, pl.ds(0, one)], ab_send_sem)
    for distance in range(parts):
        amount = one if distance == 0 else hidden
        wait_bytes(send_ab.at[0, 1, pl.ds(0, amount)], b_send_sem.at[distance])
        wait_bytes(send_ab.at[0, 1, pl.ds(0, amount)], x_send_sem.at[1, distance])
    wait_bytes(recv_x0.at[pl.ds(0, one)], x_send_sem.at[0, 0])


def local(row_total, col_total, pair_rep, residue_mask, *parameters):
    rows, cols, channels = pair_rep.shape
    hidden = parameters[2].shape[2] // 4
    parts = max(2, row_total * col_total // hidden)
    members = row_total * col_total // parts
    per_slot = hidden // members
    chunks = min(CHUNKS, per_slot)
    wide = hidden // chunks
    total = row_total * rows
    part = total // parts
    sizes = (rows, cols, hidden, row_total, col_total, parts, chunks)
    bf16, f32 = jnp.bfloat16, jnp.float32
    dma = pltpu.SemaphoreType.DMA
    arrays = (pair_rep, residue_mask.reshape(col_total, cols), *parameters)
    return pl.pallas_call(
        functools.partial(kernel, sizes),
        out_shape=jax.ShapeDtypeStruct((rows, cols, channels), f32),
        in_specs=[pl.BlockSpec(memory_space=pltpu.SMEM)]
        + [pl.BlockSpec(memory_space=pltpu.HBM)] * len(arrays),
        out_specs=pl.BlockSpec(memory_space=pltpu.VMEM),
        scratch_shapes=[pltpu.VMEM(array.shape, array.dtype) for array in arrays]
        + [
            pltpu.VMEM((2, 4 * hidden, channels), bf16),
            pltpu.VMEM((2, 4 * hidden, cols), f32),
            pltpu.VMEM((2, 2, hidden, cols), f32),
            pltpu.VMEM((rows, cols, channels), bf16),
            pltpu.VMEM((2, wide * rows, cols), f32),
            pltpu.VMEM((hidden * rows, cols), f32),
            pltpu.VMEM((rows, cols, channels), f32),
            pltpu.VMEM((2, 2, hidden, rows, cols), bf16),
            pltpu.VMEM((per_slot, part, total), bf16),
            pltpu.VMEM((per_slot, total, total), bf16),
            pltpu.VMEM((2, per_slot, part, total), bf16),
            pltpu.VMEM((per_slot, part, total), bf16),
            pltpu.VMEM((per_slot, total, total), bf16),
            pltpu.VMEM((hidden, rows, cols), bf16),
            pltpu.VMEM((parts, hidden, rows, cols), bf16),
            dma((len(arrays),)),
            dma(()),
            dma((chunks,)),
            dma((parts,)),
            dma((chunks,)),
            dma(()),
            dma((chunks,)),
            dma((2, parts)),
            dma((2, chunks)),
        ],
        compiler_params=pltpu.CompilerParams(collective_id=0, has_side_effects=True),
    )(residue_mask, *arrays)


def solution(mesh):
    return jax.shard_map(
        functools.partial(local, mesh.shape["row"], mesh.shape["ch"]),
        mesh=mesh,
        in_specs=(P("row", "ch", None), P(), P(), P(), P(), P(), P(), P(), P(), P(), P(), P()),
        out_specs=P("row", "ch", None),
        check_vma=False,
    )
```

profile of v0, /device:TPU:0, one launch (start us, length us, event | category | flops | bytes accessed | tf_op | source)
XLA Modules:
  0.0 75.6 jit_solution(2868536081023350078)
XLA Ops:
  0.0 73.3 %shard_map.118 = f32[16,128,128]{2,1,0:T(8,128)} custom-call(s32[256]{0:T(256)} %mask_smem.1, f32[16,128,128]{2,1,0:T(8,128)} %refs_0_.1, s32[2,128]{1,0:T(2,128)} %bitcast.1, f32[2,128]{1,0:T(2,128)} %refs_2_.1, f32[2,128]{1,0:T(2,128)} %refs_3_.1, bf16[2,128,512]{2,1,0:T(8,128)(2,1)} %refs_4_.1, f32[2,512]{1,0:T(2,128)} %refs_5_.1, ...), custom_call_target="tpu_custom_call" | custom-call | tf_op jit(solution)/shard_map/pallas_call | solution.py:375
  73.3 2.3 %copy.14 = f32[16,128,128]{2,1,0:T(8,128)} copy(f32[16,128,128]{2,1,0:T(8,128)} %shard_map.118) | data formatting | bytes 2097152
where the time goes:
time: 75.8 us; the launch traced here: 75.6 us
  Pallas kernels  73.3 us (97%)
  local copies, waits for them, and re-layouts  2.3 us (3%)
    pallas_call x1, Pallas kernels, local(): pl.pallas_call(functools.partial(kernel, sizes), out_shape=jax.ShapeDtype...  73.3 us
    unnamed x1, local copies, waits for them, and re-layouts  2.3 us

commit v1 on v0

--- a/solution.py
+++ b/solution.py
@@ -374,7 +374,7 @@
     arrays = (pair_rep, residue_mask.reshape(col_total, cols), *parameters)
     return pl.pallas_call(
         functools.partial(kernel, sizes),
-        out_shape=jax.ShapeDtypeStruct((rows, cols, channels), f32),
+        out_shape=pltpu.VMEM((rows, cols, channels), f32),
         in_specs=[pl.BlockSpec(memory_space=pltpu.SMEM)]
         + [pl.BlockSpec(memory_space=pltpu.HBM)] * len(arrays),
         out_specs=pl.BlockSpec(memory_space=pltpu.VMEM),

time: 75.8 us -> 73.5 us (0.970)
  local copies, waits for them, and re-layouts: 2.3 us -> 0.97 us
  Pallas kernels: 73.3 us -> 72.3 us
    unnamed x1, local copies, waits for them, and re-layouts: 2.3 us -> 0.97 us
    pallas_call x1, Pallas kernels: 73.3 us -> 72.3 us  [local(): pl.pallas_call(functools.partial(kernel, sizes), out_shape=pltpu.VMEM((ro...]
where the time goes in v1:
time: 73.5 us; the launch traced here: 73.3 us
  Pallas kernels  72.3 us (98%)
  local copies, waits for them, and re-layouts  0.97 us (1%)
    pallas_call x1, Pallas kernels, local(): pl.pallas_call(functools.partial(kernel, sizes), out_shape=pltpu.VMEM((ro...  72.3 us

profile of v1, /device:TPU:0, one launch (start us, length us, event | category | flops | bytes accessed | tf_op | source)
XLA Modules:
  0.0 73.3 jit_solution(16534917000703147613)
XLA Ops:
  0.0 72.3 %shard_map.118 = f32[16,128,128]{2,1,0:T(8,128)S(1)} custom-call(s32[256]{0:T(256)} %mask_smem.1, f32[16,128,128]{2,1,0:T(8,128)} %refs_0_.1, s32[2,128]{1,0:T(2,128)} %bitcast.1, f32[2,128]{1,0:T(2,128)} %refs_2_.1, f32[2,128]{1,0:T(2,128)} %refs_3_.1, bf16[2,128,512]{2,1,0:T(8,128)(2,1)} %refs_4_.1, f32[2,512]{1,0:T(2,128)} %refs_5_.1, ...), custom_call_target="tpu_custom_call" | custom-call | tf_op jit(solution)/shard_map/pallas_call | solution.py:375
  72.4 1.0 %copy.14 = f32[16,128,128]{2,1,0:T(8,128)} copy(f32[16,128,128]{2,1,0:T(8,128)S(1)} %shard_map.118) | data formatting | bytes 2097152

commit v2 on v1

v2 whole, which is shorter than its diff:
```python
import functools

import jax
import jax.numpy as jnp
from jax import lax
from jax.experimental import pallas as pl
from jax.experimental.pallas import tpu as pltpu
from jax.sharding import PartitionSpec as P

PAIR_EPSILON = 1e-05
HIDDEN_EPSILON = 1.0
MESH = pl.DeviceIdType.MESH
CHUNKS = 4
LEAD = 3
NAMES = (
    "pair",
    "mask",
    "pair_gain",
    "pair_shift",
    "panel_weight",
    "panel_bias",
    "gate_weight",
    "gate_bias",
    "hidden_gain",
    "hidden_shift",
    "output_weight",
    "output_bias",
)


def normalize(values, axis, epsilon, gain, shift):
    offset = values - jnp.mean(values, axis=axis, keepdims=True)
    spread = jnp.mean(offset * offset, axis=axis, keepdims=True)
    return (offset * lax.rsqrt(spread + epsilon) * gain + shift).astype(jnp.bfloat16)


def splat(line, cols):
    return jnp.broadcast_to(line, (cols, line.shape[1])).T


def turn(weight):
    return weight.astype(jnp.float32).T.astype(jnp.bfloat16)


def kernel(sizes, mask_smem, *refs):
    rows, cols, hidden, row_total, col_total, parts, chunks, halves = sizes
    count = len(NAMES)
    sources = dict(zip(NAMES, refs[:count]))
    out_ref = refs[count]
    held = dict(zip(NAMES, refs[count + 1 : 2 * count + 1]))
    (
        weight_t,
        bias_t,
        gate_t,
        output_t,
        lines_t,
        affine_t,
        normed_ref,
        stage,
        stage_x,
        pair_t,
        gate,
        send_ab0,
        send_ab1,
        recv_a,
        recv_b,
        recv_ab,
        send_x0,
        send_x1,
        recv_x0,
        recv_x1,
        load_sem,
        a_send_sem,
        a_recv_sem,
        b_send_sem,
        b_recv_sem,
        ab_send_sem,
        ab_recv_sem,
        x0_send_sem,
        x0_recv_sem,
        x1_send_sem,
        x1_recv_sem,
    ) = refs[2 * count + 1 :]
    devices = row_total * col_total
    row_part = row_total // parts
    members = row_part * col_total
    per_slot = hidden // members
    piece = per_slot // chunks
    wide = hidden // chunks
    sub = rows // halves
    tiles = piece // halves
    my_row = lax.axis_index("row")
    my_col = lax.axis_index("ch")
    my_group = my_row // row_part
    my_near = lax.rem(my_row, row_part)
    my_place = my_near * col_total + my_col

    loads = [
        pltpu.make_async_copy(sources[name], held[name], load_sem.at[at])
        for at, name in enumerate(NAMES)
    ]
    for load in loads:
        load.start()

    def partner(distance, step):
        group = lax.rem(my_group + distance, parts)
        place = lax.rem(my_place + step, members)
        return group * row_part + place // col_total, lax.rem(place, col_total), place

    def each(first, body):
        def step_body(step, carry):
            body(step)
            return carry

        steps = members - first
        unroll = max(d for d in (1, 4, 5) if steps % d == 0)
        lax.fori_loop(first, members, step_body, 0, unroll=unroll)

    barrier = pltpu.get_barrier_semaphore()
    for distance in range(parts):

        def greet(step):
            row, col, _ = partner(distance, step)
            pl.semaphore_signal(barrier, inc=1, device_id=(row, col), device_id_type=MESH)

        each(1 if distance == 0 else 0, greet)

    def wait_bytes(ref, sem):
        pltpu.make_async_copy(ref, ref, sem).wait()

    def remote(source, target, send_sem, recv_sem, row, col):
        pltpu.make_async_remote_copy(
            src_ref=source,
            dst_ref=target,
            send_sem=send_sem,
            recv_sem=recv_sem,
            device_id=(row, col),
            device_id_type=MESH,
        ).start()

    row_at = pl.multiple_of(my_row * rows, rows)
    near_at = pl.multiple_of(my_near * rows, rows)
    col_at = pl.multiple_of(my_col * cols, cols)

    def panels(chunk, place):
        return pl.ds(chunk * wide + place * piece, piece)

    def send_first_panels(chunk):
        spot = pl.ds(chunk * piece, piece)
        a_to = recv_a.at[spot, pl.ds(near_at, rows), pl.ds(col_at, cols)]
        b_to = recv_b.at[spot, pl.ds(row_at, rows), pl.ds(col_at, cols)]

        def far(distance, step):
            row, col, place = partner(distance, step)
            source = send_ab0.at[1, panels(chunk, place)]
            remote(source, b_to, b_send_sem.at[distance], b_recv_sem.at[chunk], row, col)

        def near(step):
            row, col, place = partner(0, step)
            source = send_ab0.at[0, panels(chunk, place)]
            remote(source, a_to, a_send_sem, a_recv_sem.at[chunk], row, col)

        for distance in range(parts - 1, -1, -1):
            each(1 if distance == 0 else 0, functools.partial(far, distance))
        each(1, near)
        own = panels(chunk, my_place)
        pltpu.make_async_copy(send_ab0.at[0, own], a_to, a_recv_sem.at[chunk]).start()
        pltpu.make_async_copy(send_ab0.at[1, own], b_to, b_recv_sem.at[chunk]).start()

    def send_second_panels(half, chunk):
        to = recv_ab.at[
            :, pl.ds(chunk * tiles, tiles), half, my_near, :, pl.ds(col_at, cols)
        ]

        def source_of(place):
            return send_ab1.at[:, half, pl.ds((chunk * members + place) * tiles, tiles)]

        def both(step):
            row, col, place = partner(0, step)
            remote(source_of(place), to, ab_send_sem, ab_recv_sem.at[chunk], row, col)

        each(1, both)
        pltpu.make_async_copy(source_of(my_place), to, ab_recv_sem.at[chunk]).start()

    def send_first_products(half, first, amount):
        lands = recv_x0.at[half, pl.ds(first, amount), pl.ds(my_place * tiles, tiles)]

        def source_of(row, col):
            along = pl.ds(pl.multiple_of(col * cols, cols), cols)
            return send_x0.at[
                half, pl.ds(first, amount), :, lax.rem(row, row_part), :, along
            ]

        def other(step):
            row, col, _ = partner(0, step)
            remote(source_of(row, col), lands, x0_send_sem, x0_recv_sem.at[half], row, col)

        each(1, other)
        own = source_of(my_row, my_col)
        pltpu.make_async_copy(own, lands, x0_recv_sem.at[half]).start()

    def send_second_products(chunk):
        spot = pl.ds(chunk * piece, piece)
        lands = recv_x1.at[my_group, panels(chunk, my_place)]

        def source_of(row, col):
            at = pl.ds(pl.multiple_of(row * rows, rows), rows)
            along = pl.ds(pl.multiple_of(col * cols, cols), cols)
            return send_x1.at[spot, at, along]

        def other(distance, step):
            row, col, _ = partner(distance, step)
            remote(
                source_of(row, col),
                lands,
                x1_send_sem.at[distance],
                x1_recv_sem.at[chunk],
                row,
                col,
            )

        for distance in range(parts - 1, -1, -1):
            each(1 if distance == 0 else 0, functools.partial(other, distance))
        own = source_of(my_row, my_col)
        pltpu.make_async_copy(own, lands, x1_recv_sem.at[chunk]).start()

    def prepare(section):
        for block in range(4):
            span = slice(block * hidden, (block + 1) * hidden)
            turned = turn(held["panel_weight"][section, :, span])
            biases = splat(held["panel_bias"][pl.ds(section, 1), span], cols)
            for chunk in range(chunks):
                to = pl.ds((chunk * 4 + block) * wide, wide)
                weight_t[section, to, :] = turned[chunk * wide : (chunk + 1) * wide]
                bias_t[section, to, :] = biases[chunk * wide : (chunk + 1) * wide]

    def prepare_lines():
        gate_t[...] = turn(held["gate_weight"][0])
        output_t[...] = turn(held["output_weight"][0])
        names = (("gate_bias", 0), ("output_bias", 0), ("pair_gain", 1), ("pair_shift", 1))
        for at, (name, section) in enumerate(names):
            lines_t[at] = splat(held[name][pl.ds(section, 1), :], cols)
        for section in range(2):
            for at, name in enumerate(("hidden_gain", "hidden_shift")):
                line = splat(held[name][pl.ds(section, 1), :], cols)
                affine_t[section, at] = jnp.broadcast_to(line[:, None, :], (hidden, sub, cols))

    def loop(first, steps, body):
        def step_body(r, carry):
            body(r)
            return carry

        lax.fori_loop(first, first + steps, step_body, 0, unroll=min(steps, 16))

    early = [NAMES.index(name) for name in ("pair", "pair_gain", "pair_shift")]
    for at in range(count):
        if at not in early:
            loads[at].wait()
    with jax.named_scope("prep0"):
        prepare(0)
    for at in early:
        loads[at].wait()

    def first_norm(r):
        normed_ref[r] = normalize(
            held["pair"][r],
            1,
            PAIR_EPSILON,
            held["pair_gain"][pl.ds(0, 1), :],
            held["pair_shift"][pl.ds(0, 1), :],
        )

    with jax.named_scope("norm0"):
        loop(0, rows, first_norm)
    col_mask = held["mask"][pl.ds(my_col, 1), :].astype(jnp.float32)

    def project(section, chunk, height, first, r):
        span = pl.ds(chunk * 4 * wide, 4 * wide)
        features = lax.dot_general(
            weight_t[section, span, :],
            normed_ref[r],
            (((1,), (1 - section,)), ((), ())),
            preferred_element_type=jnp.float32,
        )
        features = features + bias_t[section, span, :]
        mask = col_mask * mask_smem[my_row * rows + r].astype(jnp.float32)
        for which in range(2):
            at = 2 * which * wide
            panel = mask * jax.nn.sigmoid(features[at : at + wide])
            panel = panel * features[at + wide : at + 2 * wide]
            stage[which, pl.ds(r - first, wide, stride=height), :] = panel

    def make_first(chunk):
        loop(0, rows, functools.partial(project, 0, chunk, rows, 0))
        for which in range(2):
            send_ab0[which, pl.ds(chunk * wide, wide)] = (
                stage[which].astype(jnp.bfloat16).reshape(wide, rows, cols)
            )
        if chunk == 0:
            with jax.named_scope("barrier"):
                pl.semaphore_wait(barrier, devices - 1)
        send_first_panels(chunk)

    def make_second(half, chunk):
        loop(half * sub, sub, functools.partial(project, 1, chunk, sub, half * sub))
        for which in range(2):
            made = stage[which, pl.ds(0, wide * sub), :].astype(jnp.bfloat16)
            send_ab1[which, half, pl.ds(chunk * members * tiles, members * tiles)] = (
                made.reshape(members * tiles, rows, cols)
            )
        send_second_panels(half, chunk)

    def first_gates(r):
        pair_t[r] = held["pair"][r].T
        features = lax.dot_general(
            gate_t[...],
            normed_ref[r],
            (((1,), (1,)), ((), ())),
            preferred_element_type=jnp.float32,
        )
        gate[r] = jax.nn.sigmoid(features + lines_t[0])

    def second_gates(r):
        held["pair"][r] = pair_t[r].T
        features = lax.dot_general(
            normed_ref[r],
            held["gate_weight"][1],
            (((0,), (0,)), ((), ())),
            preferred_element_type=jnp.float32,
        )
        gate[r] = jax.nn.sigmoid(features + held["gate_bias"][pl.ds(1, 1), :])

    def multiply_first(chunk):
        spot = pl.ds(chunk * piece, piece)
        with jax.named_scope(f"waitab0_{chunk}"):
            wait_bytes(recv_a.at[spot], a_recv_sem.at[chunk])
            wait_bytes(recv_b.at[spot], b_recv_sem.at[chunk])
        for tile in range(tiles):
            products = []
            for h in range(halves):
                at = chunk * piece + tile * halves + h
                product = lax.dot_general(
                    recv_a[at],
                    recv_b[at],
                    (((1,), (1,)), ((), ())),
                    preferred_element_type=jnp.float32,
                )
                products.append(product.reshape(row_part, halves, sub, product.shape[1]))
            for half in range(halves):
                packed = jnp.concatenate([product[:, half] for product in products], axis=1)
                send_x0[half, chunk, tile] = packed.astype(jnp.bfloat16)

    def multiply_second(chunk):
        spot = pl.ds(chunk * tiles, tiles)
        with jax.named_scope(f"waitab1_{chunk}"):
            wait_bytes(recv_ab.at[:, spot], ab_recv_sem.at[chunk])
        for tile in range(tiles):
            sides = []
            for which in range(2):
                got = recv_ab[which, chunk * tiles + tile].astype(jnp.float32)
                got = got.reshape(halves * row_part, halves, sub, got.shape[-1])
                sides.append(got)
            for h in range(halves):
                left, right = (
                    side[:, h]
                    .reshape(row_part * rows, side.shape[-1])
                    .astype(jnp.bfloat16)
                    for side in sides
                )
                send_x1[chunk * piece + tile * halves + h] = lax.dot_general(
                    left,
                    right,
                    (((0,), (0,)), ((), ())),
                    preferred_element_type=jnp.float32,
                ).astype(jnp.bfloat16)
        send_second_products(chunk)

    def normalize_hidden(section, half):
        values = stage_x[half].reshape(hidden, sub, cols)
        center = jnp.sum(values, axis=0, keepdims=True) * (1.0 / hidden)
        offset = values - center
        spread = jnp.sum(offset * offset, axis=0, keepdims=True) * (1.0 / hidden)
        scale = lax.rsqrt(spread + HIDDEN_EPSILON)
        normed = offset * scale * affine_t[section, 0] + affine_t[section, 1]
        stage_x[half] = normed.reshape(hidden * sub, cols)

    def finish_first(half):
        with jax.named_scope(f"waitx0_{half}"):
            wait_bytes(recv_x0.at[half], x0_recv_sem.at[half])
        with jax.named_scope(f"finish0_{half}"):
            got = recv_x0[half].astype(jnp.float32)
            stage_x[half] = got.reshape(hidden * sub, cols)
            normalize_hidden(0, half)

            def finish(r):
                normed = stage_x[half, pl.ds(r - half * sub, hidden, stride=sub), :]
                projected = jnp.dot(
                    output_t[...],
                    normed.astype(jnp.bfloat16),
                    preferred_element_type=jnp.float32,
                )
                updated = pair_t[r] + gate[r] * (projected + lines_t[1])
                pair_t[r] = updated
                normed_ref[r] = normalize(updated, 0, PAIR_EPSILON, lines_t[2], lines_t[3])

            loop(half * sub, sub, finish)

    for chunk in range(chunks):
        with jax.named_scope(f"make0_{chunk}"):
            make_first(chunk)
    with jax.named_scope("gates0"):
        prepare_lines()
        loop(0, rows, first_gates)
        prepare(1)
    for chunk in range(chunks):
        with jax.named_scope(f"mult0_{chunk}"):
            multiply_first(chunk)
            if chunk == chunks - 2:
                send_first_products(0, 0, chunks - 1)
            if chunk == chunks - 1:
                send_first_products(0, max(chunks - 1, 0), 1)
                for half in range(1, halves):
                    send_first_products(half, 0, chunks)

    lead = min(LEAD, chunks)

    def produce(half, chunk):
        with jax.named_scope(f"make1_{half}_{chunk}"):
            make_second(half, chunk)

    early_chunks = min(2, chunks) if halves > 1 else 0
    for half in range(halves):
        finish_first(half)
        if half < halves - 1:
            for chunk in range(early_chunks):
                produce(half, chunk)
    for chunk in range(lead):
        for half in range(halves):
            if not (half < halves - 1 and chunk < early_chunks):
                produce(half, chunk)
    for chunk in range(chunks):
        with jax.named_scope(f"mult1_{chunk}"):
            multiply_second(chunk)
        if chunk + lead < chunks:
            for half in range(halves):
                produce(half, chunk + lead)
    with jax.named_scope("gates1"):
        loop(0, rows, second_gates)
    for chunk in range(chunks):
        spot = pl.ds(chunk * wide, wide)
        with jax.named_scope(f"waitx1_{chunk}"):
            wait_bytes(recv_x1.at[:, spot], x1_recv_sem.at[chunk])
        got = recv_x1[0, spot].astype(jnp.float32)
        for other in range(1, parts):
            got = got + recv_x1[other, spot].astype(jnp.float32)
        got = got.reshape(wide, halves, sub, cols)
        for half in range(halves):
            stage_x[half, pl.ds(chunk * wide * sub, wide * sub), :] = got[:, half].reshape(
                wide * sub, cols
            )

    with jax.named_scope("finish1"):
        for half in range(halves):
            normalize_hidden(1, half)

            def finish(r):
                normed = stage_x[half, pl.ds(r - half * sub, hidden, stride=sub), :]
                projected = lax.dot_general(
                    normed.astype(jnp.bfloat16),
                    held["output_weight"][1],
                    (((0,), (0,)), ((), ())),
                    preferred_element_type=jnp.float32,
                )
                projected = projected + held["output_bias"][pl.ds(1, 1), :]
                out_ref[r] = held["pair"][r] + gate[r] * projected

            loop(half * sub, sub, finish)

    one = hidden - per_slot
    wait_bytes(send_ab0.at[0, pl.ds(0, one)], a_send_sem)
    wait_bytes(send_ab1.at[:, :, pl.ds(0, one // halves)], ab_send_sem)
    for distance in range(parts):
        amount = one if distance == 0 else hidden
        wait_bytes(send_ab0.at[1, pl.ds(0, amount)], b_send_sem.at[distance])
        wait_bytes(send_ab0.at[1, pl.ds(0, amount)], x1_send_sem.at[distance])
    wait_bytes(send_ab0.at[0, pl.ds(0, one)], x0_send_sem)


def local(row_total, col_total, pair_rep, residue_mask, *parameters):
    rows, cols, channels = pair_rep.shape
    hidden = parameters[2].shape[2] // 4
    parts = max(2, row_total * col_total // hidden)
    members = row_total * col_total // parts
    row_part = row_total // parts
    per_slot = hidden // members
    chunks = min(CHUNKS, per_slot)
    piece = per_slot // chunks
    halves = 2 if piece % 2 == 0 and rows % 16 == 0 else 1
    tiles = piece // halves
    sub = rows // halves
    wide = hidden // chunks
    total = row_total * rows
    part = total // parts
    sizes = (rows, cols, hidden, row_total, col_total, parts, chunks, halves)
    bf16, f32 = jnp.bfloat16, jnp.float32
    dma = pltpu.SemaphoreType.DMA
    arrays = (pair_rep, residue_mask.reshape(col_total, cols), *parameters)
    return pl.pallas_call(
        functools.partial(kernel, sizes),
        out_shape=pltpu.VMEM((rows, cols, channels), f32),
        in_specs=[pl.BlockSpec(memory_space=pltpu.SMEM)]
        + [pl.BlockSpec(memory_space=pltpu.HBM)] * len(arrays),
        out_specs=pl.BlockSpec(memory_space=pltpu.VMEM),
        scratch_shapes=[pltpu.VMEM(array.shape, array.dtype) for array in arrays]
        + [
            pltpu.VMEM((2, 4 * hidden, channels), bf16),
            pltpu.VMEM((2, 4 * hidden, cols), f32),
            pltpu.VMEM((channels, channels), bf16),
            pltpu.VMEM((channels, hidden), bf16),
            pltpu.VMEM((4, channels, cols), f32),
            pltpu.VMEM((2, 2, hidden, sub, cols), f32),
            pltpu.VMEM((rows, cols, channels), bf16),
            pltpu.VMEM((2, wide * rows, cols), f32),
            pltpu.VMEM((halves, hidden * sub, cols), f32),
            pltpu.VMEM((rows, channels, cols), f32),
            pltpu.VMEM((rows, cols, channels), f32),
            pltpu.VMEM((2, hidden, rows, cols), bf16),
            pltpu.VMEM((2, halves, hidden // halves, rows, cols), bf16),
            pltpu.VMEM((per_slot, part, total), bf16),
            pltpu.VMEM((per_slot, total, total), bf16),
            pltpu.VMEM((2, per_slot // halves, halves, row_part, rows, total), bf16),
            pltpu.VMEM((halves, chunks, tiles, row_part, rows, total), bf16),
            pltpu.VMEM((per_slot, total, total), bf16),
            pltpu.VMEM((halves, chunks, members * tiles, rows, cols), bf16),
            pltpu.VMEM((parts, hidden, rows, cols), bf16),
            dma((len(arrays),)),
            dma(()),
            dma((chunks,)),
            dma((parts,)),
            dma((chunks,)),
            dma(()),
            dma((chunks,)),
            dma(()),
            dma((halves,)),
            dma((parts,)),
            dma((chunks,)),
        ],
        compiler_params=pltpu.CompilerParams(collective_id=0, has_side_effects=True),
    )(residue_mask, *arrays)


def solution(mesh):
    return jax.shard_map(
        functools.partial(local, mesh.shape["row"], mesh.shape["ch"]),
        mesh=mesh,
        in_specs=(P("row", "ch", None), P(), P(), P(), P(), P(), P(), P(), P(), P(), P(), P()),
        out_specs=P("row", "ch", None),
        check_vma=False,
    )
```

time: 73.5 us -> 73.9 us (level)
  no operation moved by 1% of the time
where the time goes in v2:
time: 73.9 us; the launch traced here: 73.7 us
  Pallas kernels  72.7 us (98%)
  local copies, waits for them, and re-layouts  0.97 us (1%)
    pallas_call x1, Pallas kernels, local(): pl.pallas_call(functools.partial(kernel, sizes), out_shape=pltpu.VMEM((ro...  72.7 us

profile of v2, /device:TPU:0, one launch (start us, length us, event | category | flops | bytes accessed | tf_op | source)
XLA Modules:
  0.0 73.7 jit_solution(11888448562467179216)
XLA Ops:
  0.0 72.7 %shard_map.118 = f32[16,128,128]{2,1,0:T(8,128)S(1)} custom-call(s32[256]{0:T(256)} %mask_smem.1, f32[16,128,128]{2,1,0:T(8,128)} %refs_0_.1, s32[2,128]{1,0:T(2,128)} %bitcast.1, f32[2,128]{1,0:T(2,128)} %refs_2_.1, f32[2,128]{1,0:T(2,128)} %refs_3_.1, bf16[2,128,512]{2,1,0:T(8,128)(2,1)} %refs_4_.1, f32[2,512]{1,0:T(2,128)} %refs_5_.1, ...), custom_call_target="tpu_custom_call" | custom-call | tf_op jit(solution)/shard_map/pallas_call | solution.py:508
  72.7 1.0 %copy.14 = f32[16,128,128]{2,1,0:T(8,128)} copy(f32[16,128,128]{2,1,0:T(8,128)S(1)} %shard_map.118) | data formatting | bytes 2097152

commit v3 on v2

--- a/solution.py
+++ b/solution.py
@@ -42,7 +42,7 @@
     return weight.astype(jnp.float32).T.astype(jnp.bfloat16)
 
 
-def kernel(sizes, mask_smem, *refs):
+def kernel(sizes, mask_hbm, *refs):
     rows, cols, hidden, row_total, col_total, parts, chunks, halves = sizes
     count = len(NAMES)
     sources = dict(zip(NAMES, refs[:count]))
@@ -80,6 +80,8 @@
         x0_recv_sem,
         x1_send_sem,
         x1_recv_sem,
+        mask_smem,
+        mask_sem,
     ) = refs[2 * count + 1 :]
     devices = row_total * col_total
     row_part = row_total // parts
@@ -99,8 +101,15 @@
         pltpu.make_async_copy(sources[name], held[name], load_sem.at[at])
         for at, name in enumerate(NAMES)
     ]
-    for load in loads:
-        load.start()
+    order = ("panel_weight", "pair_gain", "pair_shift", "panel_bias", "mask", "pair")
+    urgent = [NAMES.index(name) for name in order]
+    later = [at for at in range(count) if at not in urgent]
+    mask_load = pltpu.make_async_copy(mask_hbm, mask_smem, mask_sem)
+    for at in urgent:
+        loads[at].start()
+    mask_load.start()
+    for at in later:
+        loads[at].start()
 
     def partner(distance, step):
         group = lax.rem(my_group + distance, parts)
@@ -145,27 +154,39 @@
     def panels(chunk, place):
         return pl.ds(chunk * wide + place * piece, piece)
 
-    def send_first_panels(chunk):
+    def first_targets(chunk):
         spot = pl.ds(chunk * piece, piece)
         a_to = recv_a.at[spot, pl.ds(near_at, rows), pl.ds(col_at, cols)]
         b_to = recv_b.at[spot, pl.ds(row_at, rows), pl.ds(col_at, cols)]
-
-        def far(distance, step):
+        return a_to, b_to
+
+    def send_right(distance, chunk):
+        _, b_to = first_targets(chunk)
+
+        def right(step):
             row, col, place = partner(distance, step)
             source = send_ab0.at[1, panels(chunk, place)]
             remote(source, b_to, b_send_sem.at[distance], b_recv_sem.at[chunk], row, col)
 
-        def near(step):
+        each(1 if distance == 0 else 0, right)
+
+    def send_near_panels(chunk):
+        a_to, b_to = first_targets(chunk)
+
+        def left(step):
             row, col, place = partner(0, step)
             source = send_ab0.at[0, panels(chunk, place)]
             remote(source, a_to, a_send_sem, a_recv_sem.at[chunk], row, col)
 
-        for distance in range(parts - 1, -1, -1):
-            each(1 if distance == 0 else 0, functools.partial(far, distance))
-        each(1, near)
+        send_right(0, chunk)
+        each(1, left)
         own = panels(chunk, my_place)
         pltpu.make_async_copy(send_ab0.at[0, own], a_to, a_recv_sem.at[chunk]).start()
         pltpu.make_async_copy(send_ab0.at[1, own], b_to, b_recv_sem.at[chunk]).start()
+
+    def send_far_panels(chunk):
+        for distance in range(parts - 1, 0, -1):
+            send_right(distance, chunk)
 
     def send_second_panels(half, chunk):
         to = recv_ab.at[
@@ -239,7 +260,7 @@
         output_t[...] = turn(held["output_weight"][0])
         names = (("gate_bias", 0), ("output_bias", 0), ("pair_gain", 1), ("pair_shift", 1))
         for at, (name, section) in enumerate(names):
-            lines_t[at] = splat(held[name][pl.ds(section, 1), :], cols)
+            lines_t[2 + at] = splat(held[name][pl.ds(section, 1), :], cols)
         for section in range(2):
             for at, name in enumerate(("hidden_gain", "hidden_shift")):
                 line = splat(held[name][pl.ds(section, 1), :], cols)
@@ -252,23 +273,19 @@
 
         lax.fori_loop(first, first + steps, step_body, 0, unroll=min(steps, 16))
 
-    early = [NAMES.index(name) for name in ("pair", "pair_gain", "pair_shift")]
-    for at in range(count):
-        if at not in early:
-            loads[at].wait()
+    for at in urgent[:-1]:
+        loads[at].wait()
     with jax.named_scope("prep0"):
+        for at, name in enumerate(("pair_gain", "pair_shift")):
+            lines_t[at] = splat(held[name][pl.ds(0, 1), :], cols)
         prepare(0)
-    for at in early:
-        loads[at].wait()
+    mask_load.wait()
+    loads[urgent[-1]].wait()
 
     def first_norm(r):
-        normed_ref[r] = normalize(
-            held["pair"][r],
-            1,
-            PAIR_EPSILON,
-            held["pair_gain"][pl.ds(0, 1), :],
-            held["pair_shift"][pl.ds(0, 1), :],
-        )
+        values = held["pair"][r].T
+        pair_t[r] = values
+        normed_ref[r] = normalize(values, 0, PAIR_EPSILON, lines_t[0], lines_t[1])
 
     with jax.named_scope("norm0"):
         loop(0, rows, first_norm)
@@ -279,7 +296,7 @@
         features = lax.dot_general(
             weight_t[section, span, :],
             normed_ref[r],
-            (((1,), (1 - section,)), ((), ())),
+            (((1,), (0,)), ((), ())),
             preferred_element_type=jnp.float32,
         )
         features = features + bias_t[section, span, :]
@@ -299,7 +316,8 @@
         if chunk == 0:
             with jax.named_scope("barrier"):
                 pl.semaphore_wait(barrier, devices - 1)
-        send_first_panels(chunk)
+        send_far_panels(chunk)
+        send_near_panels(chunk)
 
     def make_second(half, chunk):
         loop(half * sub, sub, functools.partial(project, 1, chunk, sub, half * sub))
@@ -311,14 +329,8 @@
         send_second_panels(half, chunk)
 
     def first_gates(r):
-        pair_t[r] = held["pair"][r].T
-        features = lax.dot_general(
-            gate_t[...],
-            normed_ref[r],
-            (((1,), (1,)), ((), ())),
-            preferred_element_type=jnp.float32,
-        )
-        gate[r] = jax.nn.sigmoid(features + lines_t[0])
+        features = jnp.dot(gate_t[...], normed_ref[r], preferred_element_type=jnp.float32)
+        gate[r] = jax.nn.sigmoid(features + lines_t[2])
 
     def second_gates(r):
         held["pair"][r] = pair_t[r].T
@@ -399,15 +411,17 @@
                     normed.astype(jnp.bfloat16),
                     preferred_element_type=jnp.float32,
                 )
-                updated = pair_t[r] + gate[r] * (projected + lines_t[1])
+                updated = pair_t[r] + gate[r] * (projected + lines_t[3])
                 pair_t[r] = updated
-                normed_ref[r] = normalize(updated, 0, PAIR_EPSILON, lines_t[2], lines_t[3])
+                normed_ref[r] = normalize(updated, 0, PAIR_EPSILON, lines_t[4], lines_t[5])
 
             loop(half * sub, sub, finish)
 
     for chunk in range(chunks):
         with jax.named_scope(f"make0_{chunk}"):
             make_first(chunk)
+    for at in later:
+        loads[at].wait()
     with jax.named_scope("gates0"):
         prepare_lines()
         loop(0, rows, first_gates)
@@ -417,10 +431,11 @@
             multiply_first(chunk)
             if chunk == chunks - 2:
                 send_first_products(0, 0, chunks - 1)
+                for half in range(1, halves):
+                    send_first_products(half, 0, chunks - 1)
             if chunk == chunks - 1:
-                send_first_products(0, max(chunks - 1, 0), 1)
-                for half in range(1, halves):
-                    send_first_products(half, 0, chunks)
+                for half in range(halves):
+                    send_first_products(half, chunk, 1)
 
     lead = min(LEAD, chunks)
 
@@ -428,7 +443,7 @@
         with jax.named_scope(f"make1_{half}_{chunk}"):
             make_second(half, chunk)
 
-    early_chunks = min(2, chunks) if halves > 1 else 0
+    early_chunks = min(1, chunks) if halves > 1 else 0
     for half in range(halves):
         finish_first(half)
         if half < halves - 1:
@@ -508,8 +523,7 @@
     return pl.pallas_call(
         functools.partial(kernel, sizes),
         out_shape=pltpu.VMEM((rows, cols, channels), f32),
-        in_specs=[pl.BlockSpec(memory_space=pltpu.SMEM)]
-        + [pl.BlockSpec(memory_space=pltpu.HBM)] * len(arrays),
+        in_specs=[pl.BlockSpec(memory_space=pltpu.HBM)] * (1 + len(arrays)),
         out_specs=pl.BlockSpec(memory_space=pltpu.VMEM),
         scratch_shapes=[pltpu.VMEM(array.shape, array.dtype) for array in arrays]
         + [
@@ -517,9 +531,9 @@
             pltpu.VMEM((2, 4 * hidden, cols), f32),
             pltpu.VMEM((channels, channels), bf16),
             pltpu.VMEM((channels, hidden), bf16),
-            pltpu.VMEM((4, channels, cols), f32),
+            pltpu.VMEM((6, channels, cols), f32),
             pltpu.VMEM((2, 2, hidden, sub, cols), f32),
-            pltpu.VMEM((rows, cols, channels), bf16),
+            pltpu.VMEM((rows, channels, cols), bf16),
             pltpu.VMEM((2, wide * rows, cols), f32),
             pltpu.VMEM((halves, hidden * sub, cols), f32),
             pltpu.VMEM((rows, channels, cols), f32),
@@ -544,6 +558,8 @@
             dma((halves,)),
             dma((parts,)),
             dma((chunks,)),
+            pltpu.SMEM(residue_mask.shape, residue_mask.dtype),
+            dma(()),
         ],
         compiler_params=pltpu.CompilerParams(collective_id=0, has_side_effects=True),
     )(residue_mask, *arrays)

time: 73.9 us -> 71.2 us (0.963)
  Pallas kernels: 72.7 us -> 70.1 us
    pallas_call x1, Pallas kernels: 72.7 us -> 70.1 us  [local(): pl.pallas_call(functools.partial(kernel, sizes), out_shape=pltpu.VMEM((ro...]
where the time goes in v3:
time: 71.2 us; the launch traced here: 71 us
  Pallas kernels  70.1 us (98%)
  local copies, waits for them, and re-layouts  0.97 us (1%)
    pallas_call x1, Pallas kernels, local(): pl.pallas_call(functools.partial(kernel, sizes), out_shape=pltpu.VMEM((ro...  70.1 us

profile of v3, /device:TPU:0, one launch (start us, length us, event | category | flops | bytes accessed | tf_op | source)
XLA Modules:
  0.0 71.0 jit_solution(6313741979319180227)
XLA Ops:
  0.0 70.1 %shard_map.118 = f32[16,128,128]{2,1,0:T(8,128)S(1)} custom-call(s32[256]{0:T(256)} %mask_hbm.1, f32[16,128,128]{2,1,0:T(8,128)} %refs_0_.1, s32[2,128]{1,0:T(2,128)} %bitcast.1, f32[2,128]{1,0:T(2,128)} %refs_2_.1, f32[2,128]{1,0:T(2,128)} %refs_3_.1, bf16[2,128,512]{2,1,0:T(8,128)(2,1)} %refs_4_.1, f32[2,512]{1,0:T(2,128)} %refs_5_.1, ...), custom_call_target="tpu_custom_call" | custom-call | tf_op jit(solution)/shard_map/pallas_call | solution.py:523
  70.1 1.0 %copy.14 = f32[16,128,128]{2,1,0:T(8,128)} copy(f32[16,128,128]{2,1,0:T(8,128)S(1)} %shard_map.118) | data formatting | bytes 2097152

commit v4 on v3

--- a/solution.py
+++ b/solution.py
@@ -11,7 +11,7 @@
 HIDDEN_EPSILON = 1.0
 MESH = pl.DeviceIdType.MESH
 CHUNKS = 4
-LEAD = 3
+LEAD = 4
 NAMES = (
     "pair",
     "mask",
@@ -220,7 +220,7 @@
         own = source_of(my_row, my_col)
         pltpu.make_async_copy(own, lands, x0_recv_sem.at[half]).start()
 
-    def send_second_products(chunk):
+    def send_second_products(chunk, near):
         spot = pl.ds(chunk * piece, piece)
         lands = recv_x1.at[my_group, panels(chunk, my_place)]
 
@@ -240,8 +240,11 @@
                 col,
             )
 
-        for distance in range(parts - 1, -1, -1):
-            each(1 if distance == 0 else 0, functools.partial(other, distance))
+        if not near:
+            for distance in range(parts - 1, 0, -1):
+                each(0, functools.partial(other, distance))
+            return
+        each(1, functools.partial(other, 0))
         own = source_of(my_row, my_col)
         pltpu.make_async_copy(own, lands, x1_recv_sem.at[chunk]).start()
 
@@ -385,24 +388,43 @@
                     (((0,), (0,)), ((), ())),
                     preferred_element_type=jnp.float32,
                 ).astype(jnp.bfloat16)
-        send_second_products(chunk)
-
-    def normalize_hidden(section, half):
-        values = stage_x[half].reshape(hidden, sub, cols)
-        center = jnp.sum(values, axis=0, keepdims=True) * (1.0 / hidden)
-        offset = values - center
-        spread = jnp.sum(offset * offset, axis=0, keepdims=True) * (1.0 / hidden)
-        scale = lax.rsqrt(spread + HIDDEN_EPSILON)
-        normed = offset * scale * affine_t[section, 0] + affine_t[section, 1]
-        stage_x[half] = normed.reshape(hidden * sub, cols)
+        send_second_products(chunk, False)
+
+    strip = min(hidden, 16)
+
+    def strips(half):
+        for at in range(0, hidden, strip):
+            spot = pl.ds(at * sub, strip * sub)
+            yield at, spot, stage_x[half, spot, :].reshape(strip, sub, cols)
+
+    def fill(half, at, values):
+        stage_x[half, pl.ds(at * sub, values.shape[0] * sub), :] = values.reshape(-1, cols)
+        return jnp.sum(values, axis=0)
+
+    def normalize_hidden(section, half, summed):
+        center = summed * (1.0 / hidden)
+        spread = jnp.zeros((sub, cols), jnp.float32)
+        for _, _, values in strips(half):
+            offset = values - center
+            spread = spread + jnp.sum(offset * offset, axis=0)
+        scale = lax.rsqrt(spread * (1.0 / hidden) + HIDDEN_EPSILON)
+        for at, spot, values in strips(half):
+            normed = (values - center) * scale * affine_t[section, 0, pl.ds(at, strip)]
+            normed = normed + affine_t[section, 1, pl.ds(at, strip)]
+            stage_x[half, spot, :] = normed.reshape(strip * sub, cols)
 
     def finish_first(half):
         with jax.named_scope(f"waitx0_{half}"):
             wait_bytes(recv_x0.at[half], x0_recv_sem.at[half])
         with jax.named_scope(f"finish0_{half}"):
-            got = recv_x0[half].astype(jnp.float32)
-            stage_x[half] = got.reshape(hidden * sub, cols)
-            normalize_hidden(0, half)
+            summed = jnp.zeros((sub, cols), jnp.float32)
+            for chunk in range(chunks):
+                for at in range(0, members * tiles, strip // halves):
+                    height = min(strip // halves, members * tiles)
+                    got = recv_x0[half, chunk, pl.ds(at, height)].astype(jnp.float32)
+                    got = got.reshape(height * halves, sub, cols)
+                    summed = summed + fill(half, chunk * wide + at * halves, got)
+            normalize_hidden(0, half, summed)
 
             def finish(r):
                 normed = stage_x[half, pl.ds(r - half * sub, hidden, stride=sub), :]
@@ -459,24 +481,28 @@
         if chunk + lead < chunks:
             for half in range(halves):
                 produce(half, chunk + lead)
+        if chunk >= 1:
+            send_second_products(chunk - 1, True)
+    for chunk in range(chunks - 1, chunks):
+        send_second_products(chunk, True)
     with jax.named_scope("gates1"):
         loop(0, rows, second_gates)
+    summed = [jnp.zeros((sub, cols), jnp.float32) for _ in range(halves)]
     for chunk in range(chunks):
-        spot = pl.ds(chunk * wide, wide)
         with jax.named_scope(f"waitx1_{chunk}"):
-            wait_bytes(recv_x1.at[:, spot], x1_recv_sem.at[chunk])
-        got = recv_x1[0, spot].astype(jnp.float32)
-        for other in range(1, parts):
-            got = got + recv_x1[other, spot].astype(jnp.float32)
-        got = got.reshape(wide, halves, sub, cols)
-        for half in range(halves):
-            stage_x[half, pl.ds(chunk * wide * sub, wide * sub), :] = got[:, half].reshape(
-                wide * sub, cols
-            )
+            wait_bytes(recv_x1.at[:, pl.ds(chunk * wide, wide)], x1_recv_sem.at[chunk])
+        for at in range(chunk * wide, (chunk + 1) * wide, min(strip, wide)):
+            height = min(strip, wide)
+            got = recv_x1[0, pl.ds(at, height)].astype(jnp.float32)
+            for other in range(1, parts):
+                got = got + recv_x1[other, pl.ds(at, height)].astype(jnp.float32)
+            got = got.reshape(height, halves, sub, cols)
+            for half in range(halves):
+                summed[half] = summed[half] + fill(half, at, got[:, half])
 
     with jax.named_scope("finish1"):
         for half in range(halves):
-            normalize_hidden(1, half)
+            normalize_hidden(1, half, summed[half])
 
             def finish(r):
                 normed = stage_x[half, pl.ds(r - half * sub, hidden, stride=sub), :]

time: 71.2 us -> 70.9 us (level)
  no operation moved by 1% of the time
where the time goes in v4:
time: 70.9 us; the launch traced here: 70.7 us
  Pallas kernels  69.8 us (98%)
  local copies, waits for them, and re-layouts  0.97 us (1%)
    pallas_call x1, Pallas kernels, local(): pl.pallas_call(functools.partial(kernel, sizes), out_shape=pltpu.VMEM((ro...  69.8 us

profile of v4, /device:TPU:0, one launch (start us, length us, event | category | flops | bytes accessed | tf_op | source)
XLA Modules:
  0.0 70.7 jit_solution(9085399505957902714)
XLA Ops:
  0.0 69.8 %shard_map.118 = f32[16,128,128]{2,1,0:T(8,128)S(1)} custom-call(s32[256]{0:T(256)} %mask_hbm.1, f32[16,128,128]{2,1,0:T(8,128)} %refs_0_.1, s32[2,128]{1,0:T(2,128)} %bitcast.1, f32[2,128]{1,0:T(2,128)} %refs_2_.1, f32[2,128]{1,0:T(2,128)} %refs_3_.1, bf16[2,128,512]{2,1,0:T(8,128)(2,1)} %refs_4_.1, f32[2,512]{1,0:T(2,128)} %refs_5_.1, ...), custom_call_target="tpu_custom_call" | custom-call | tf_op jit(solution)/shard_map/pallas_call | solution.py:549
  69.8 1.0 %copy.14 = f32[16,128,128]{2,1,0:T(8,128)} copy(f32[16,128,128]{2,1,0:T(8,128)S(1)} %shard_map.118) | data formatting | bytes 2097152

commit v5 on v4

--- a/solution.py
+++ b/solution.py
@@ -113,7 +113,11 @@
 
     def partner(distance, step):
         group = lax.rem(my_group + distance, parts)
-        place = lax.rem(my_place + step, members)
+        if members & (members - 1):
+            place = lax.rem(my_place + step, members)
+        else:
+            reach = members - step if distance == 0 else members - 1 - step
+            place = my_place ^ reach
         return group * row_part + place // col_total, lax.rem(place, col_total), place
 
     def each(first, body):
@@ -294,8 +298,8 @@
         loop(0, rows, first_norm)
     col_mask = held["mask"][pl.ds(my_col, 1), :].astype(jnp.float32)
 
-    def project(section, chunk, height, first, r):
-        span = pl.ds(chunk * 4 * wide, 4 * wide)
+    def project(section, chunk, height, first, r, sides=(0, 1)):
+        span = pl.ds((chunk * 4 + 2 * sides[0]) * wide, 2 * len(sides) * wide)
         features = lax.dot_general(
             weight_t[section, span, :],
             normed_ref[r],
@@ -304,22 +308,24 @@
         )
         features = features + bias_t[section, span, :]
         mask = col_mask * mask_smem[my_row * rows + r].astype(jnp.float32)
-        for which in range(2):
-            at = 2 * which * wide
+        for which in sides:
+            at = 2 * (which - sides[0]) * wide
             panel = mask * jax.nn.sigmoid(features[at : at + wide])
             panel = panel * features[at + wide : at + 2 * wide]
             stage[which, pl.ds(r - first, wide, stride=height), :] = panel
 
     def make_first(chunk):
-        loop(0, rows, functools.partial(project, 0, chunk, rows, 0))
-        for which in range(2):
-            send_ab0[which, pl.ds(chunk * wide, wide)] = (
-                stage[which].astype(jnp.bfloat16).reshape(wide, rows, cols)
-            )
-        if chunk == 0:
-            with jax.named_scope("barrier"):
-                pl.semaphore_wait(barrier, devices - 1)
-        send_far_panels(chunk)
+        for sides in ((1,), (0,)) if chunk == 0 else ((0, 1),):
+            loop(0, rows, functools.partial(project, 0, chunk, rows, 0, sides=sides))
+            for which in sides:
+                send_ab0[which, pl.ds(chunk * wide, wide)] = (
+                    stage[which].astype(jnp.bfloat16).reshape(wide, rows, cols)
+                )
+            if sides == (1,):
+                with jax.named_scope("barrier"):
+                    pl.semaphore_wait(barrier, devices - 1)
+            if 1 in sides:
+                send_far_panels(chunk)
         send_near_panels(chunk)
 
     def make_second(half, chunk):
@@ -336,14 +342,15 @@
         gate[r] = jax.nn.sigmoid(features + lines_t[2])
 
     def second_gates(r):
-        held["pair"][r] = pair_t[r].T
         features = lax.dot_general(
             normed_ref[r],
             held["gate_weight"][1],
             (((0,), (0,)), ((), ())),
             preferred_element_type=jnp.float32,
         )
-        gate[r] = jax.nn.sigmoid(features + held["gate_bias"][pl.ds(1, 1), :])
+        value = jax.nn.sigmoid(features + held["gate_bias"][pl.ds(1, 1), :])
+        gate[r] = value
+        held["pair"][r] = pair_t[r].T + value * held["output_bias"][pl.ds(1, 1), :]
 
     def multiply_first(chunk):
         spot = pl.ds(chunk * piece, piece)
@@ -512,7 +519,6 @@
                     (((0,), (0,)), ((), ())),
                     preferred_element_type=jnp.float32,
                 )
-                projected = projected + held["output_bias"][pl.ds(1, 1), :]
                 out_ref[r] = held["pair"][r] + gate[r] * projected
 
             loop(half * sub, sub, finish)

time: 70.9 us -> 70.9 us (level)
  no operation moved by 1% of the time
where the time goes in v5:
time: 70.9 us; the launch traced here: 70.8 us
  Pallas kernels  69.8 us (98%)
  local copies, waits for them, and re-layouts  0.97 us (1%)
    pallas_call x1, Pallas kernels, local(): pl.pallas_call(functools.partial(kernel, sizes), out_shape=pltpu.VMEM((ro...  69.8 us

profile of v5, /device:TPU:0, one launch (start us, length us, event | category | flops | bytes accessed | tf_op | source)
XLA Modules:
  0.0 70.8 jit_solution(11565636406905448784)
XLA Ops:
  0.0 69.8 %shard_map.118 = f32[16,128,128]{2,1,0:T(8,128)S(1)} custom-call(s32[256]{0:T(256)} %mask_hbm.1, f32[16,128,128]{2,1,0:T(8,128)} %refs_0_.1, s32[2,128]{1,0:T(2,128)} %bitcast.1, f32[2,128]{1,0:T(2,128)} %refs_2_.1, f32[2,128]{1,0:T(2,128)} %refs_3_.1, bf16[2,128,512]{2,1,0:T(8,128)(2,1)} %refs_4_.1, f32[2,512]{1,0:T(2,128)} %refs_5_.1, ...), custom_call_target="tpu_custom_call" | custom-call | tf_op jit(solution)/shard_map/pallas_call | solution.py:555
  69.8 1.0 %copy.14 = f32[16,128,128]{2,1,0:T(8,128)} copy(f32[16,128,128]{2,1,0:T(8,128)S(1)} %shard_map.118) | data formatting | bytes 2097152

commit v6 on v5

--- a/solution.py
+++ b/solution.py
@@ -458,13 +458,8 @@
     for chunk in range(chunks):
         with jax.named_scope(f"mult0_{chunk}"):
             multiply_first(chunk)
-            if chunk == chunks - 2:
-                send_first_products(0, 0, chunks - 1)
-                for half in range(1, halves):
-                    send_first_products(half, 0, chunks - 1)
-            if chunk == chunks - 1:
-                for half in range(halves):
-                    send_first_products(half, chunk, 1)
+            for half in range(halves):
+                send_first_products(half, chunk, 1)
 
     lead = min(LEAD, chunks)
 

time: 70.9 us -> 70.9 us (level)
  no operation moved by 1% of the time
where the time goes in v6:
time: 70.9 us; the launch traced here: 70.8 us
  Pallas kernels  69.8 us (98%)
  local copies, waits for them, and re-layouts  0.97 us (1%)
    pallas_call x1, Pallas kernels, local(): pl.pallas_call(functools.partial(kernel, sizes), out_shape=pltpu.VMEM((ro...  69.8 us

profile of v6, /device:TPU:0, one launch (start us, length us, event | category | flops | bytes accessed | tf_op | source)
XLA Modules:
  0.0 70.8 jit_solution(15058854890219150691)
XLA Ops:
  0.0 69.8 %shard_map.118 = f32[16,128,128]{2,1,0:T(8,128)S(1)} custom-call(s32[256]{0:T(256)} %mask_hbm.1, f32[16,128,128]{2,1,0:T(8,128)} %refs_0_.1, s32[2,128]{1,0:T(2,128)} %bitcast.1, f32[2,128]{1,0:T(2,128)} %refs_2_.1, f32[2,128]{1,0:T(2,128)} %refs_3_.1, bf16[2,128,512]{2,1,0:T(8,128)(2,1)} %refs_4_.1, f32[2,512]{1,0:T(2,128)} %refs_5_.1, ...), custom_call_target="tpu_custom_call" | custom-call | tf_op jit(solution)/shard_map/pallas_call | solution.py:550
  69.8 1.0 %copy.14 = f32[16,128,128]{2,1,0:T(8,128)} copy(f32[16,128,128]{2,1,0:T(8,128)S(1)} %shard_map.118) | data formatting | bytes 2097152
